TPU v7x, 128 devices: a whole 4x4x4 slice. The times are simulated.
128 devices in a mesh: space: 16 (over z_lo, y, core), mode: 8 (over x, z_hi).
Axes of the slice: x: 4, y: 4, z: 4 (z_hi: 2, z_lo: 2; z = z_hi * 2 + z_lo), core: 2. Of those that a mesh axis runs over, the one named last changes fastest.
Arguments:
- test_modes: float32 [32, 3, 8, 32, 256], P(None, None, None, 'space'), may hold values from -6 to 6
- modes: float32 [128, 3, 8, 32, 256], P('mode', None, None, 'space'), may hold values from -6 to 6
Outputs:
- triad: float32 [32, 128, 128], P('space', 'mode')
All inputs are finite; a program needn't handle non-finite values.
Results may differ from a plain program's by a relative error of at most 0.000071.
Values sent between devices are 32-bit elements; how exact they have to be, the bound alone decides.
A program may use at most 64 MiB of HBM per device.

v0:
```python
import math
import jax
import jax.numpy as jnp
from jax import lax
from jax.sharding import PartitionSpec as P

MODES = 128
NX = 256
NZ = 8
BLOCK = 2048


def extended(value, sides, width):
    for axis, dim in sides:
        size, length = (lax.axis_size(axis), value.shape[dim])
        up = [(i, (i + 1) % size) for i in range(size)]
        down = [(j, i) for i, j in up]
        last = lax.slice_in_dim(value, length - width, length, axis=dim)
        leading = lax.slice_in_dim(value, 0, width, axis=dim)
        before = lax.ppermute(last, axis, up)
        after = lax.ppermute(leading, axis, down)
        value = jnp.concatenate([before, value, after], axis=dim)
    return value


def in_blocks(value, dim, size):
    shape = value.shape
    parts = value.reshape(*shape[:dim], size, shape[dim] // size, *shape[dim + 1 :])
    return jnp.moveaxis(parts, dim, 0)


def sent_and_summed(value, axis, dim):
    parts = in_blocks(value, dim, lax.axis_size(axis))
    arrived = lax.all_to_all(parts, axis, split_axis=0, concat_axis=0, tiled=True)
    return arrived.sum(axis=0)


def central_diff(field, along):
    ahead = jnp.roll(field, -1, along) - jnp.roll(field, 1, along)
    farther = jnp.roll(field, -2, along) - jnp.roll(field, 2, along)
    return (8.0 * ahead - farther) / 12.0


def per_device(test_modes, modes):
    local_count = modes.shape[0]
    test_count = test_modes.shape[0]
    row_count = modes.shape[3]
    padded = extended(modes, (("space", 3),), 2)
    ahead = padded[:, :, :, 3 : row_count + 3] - padded[:, :, :, 1 : row_count + 1]
    farther = padded[:, :, :, 4 : row_count + 4] - padded[:, :, :, 0:row_count]
    along_y = (8.0 * ahead - farther) / 12.0
    gradients = jnp.stack([central_diff(modes, 4), along_y, central_diff(modes, 2)], axis=2)
    gradients = gradients.reshape(local_count, 3, 3, -1)
    test_flat = test_modes.reshape(test_count, 3, -1)
    mode_flat = modes.reshape(local_count, 3, -1)
    cell_count = test_flat.shape[2]
    block_count = cell_count // BLOCK
    volume_scale = 1.0 / math.sqrt(NX * NZ * row_count * lax.axis_size("space"))

    def weigh(offset):
        test_block = lax.dynamic_slice_in_dim(test_flat, offset, BLOCK, 2)
        grad_block = lax.dynamic_slice_in_dim(gradients, offset, BLOCK, 3)
        weighted = test_block[:, 0, None, None, :] * grad_block[None, :, 0]
        weighted = weighted + test_block[:, 1, None, None, :] * grad_block[None, :, 1]
        weighted = weighted + test_block[:, 2, None, None, :] * grad_block[None, :, 2]
        return weighted

    def add_piece(running, weighted, piece_block):
        partial_value = jnp.einsum(
            "ikbc,jbc->ikj", weighted, piece_block, precision=lax.Precision.HIGHEST
        )
        return running + partial_value

    initial = jnp.zeros((test_count, local_count, MODES), jnp.float32)
    everything = lax.all_gather(mode_flat, "mode", axis=0, tiled=True)

    def one_block(index_block, running):
        offset = index_block * BLOCK
        weighted = weigh(offset)
        piece_block = lax.dynamic_slice_in_dim(everything, offset, BLOCK, 2)
        return add_piece(running, weighted, piece_block)

    partial_triad = lax.fori_loop(0, block_count, one_block, initial)
    partial_triad = partial_triad * volume_scale
    result = sent_and_summed(partial_triad, "space", 0)
    return result


def solution(mesh):
    in_specs = (P(None, None, None, "space", None), P("mode", None, None, "space", None))
    out_specs = P("space", "mode", None)
    return jax.shard_map(
        per_device, mesh=mesh, in_specs=in_specs, out_specs=out_specs, check_vma=False
    )
```

profile of v0, /device:TPU:1, one launch (start us, length us, event | category | flops | bytes accessed | tf_op | source)
XLA Modules:
  0.0 155.8 jit_solution(17726550223214487848)
XLA Ops:
  6.5 0.0 copy-start
  6.5 0.0 all-gather.2.cloned.1.call-start
  6.5 1.5 copy.22
  8.1 1.6 %reshape.137 = f32[16,3,4096]{2,0,1:T(8,128)} reshape(f32[16,3,8,2,256]{4,3,2,0,1:T(2,128)S(1)} %copy.22) | data formatting | bytes 1572864 | tf_op jit(solution)/shard_map/reshape | solution.py:55
  9.7 0.0 all-gather.2.cloned.1.call-update
  9.7 1.5 collective-permute-start
  11.1 1.4 collective-permute-start.1
  12.5 1.6 %fusion.35 = (f32[16,3,8,2,1]{4,3,2,1,0:T(2,128)S(1)}, f32[16,3,8,2,1]{4,3,2,1,0:T(2,128)S(1)}) fusion(f32[16,3,8,2,256]{4,3,2,1,0:T(2,128)} %param.5), kind=kLoop, calls=%fused_computation.55 | loop fusion | bytes 12288 | tf_op jit(solution)/shard_map/jit(_roll_static)/slice | solution.py:39
  14.1 0.4 copy.24
  14.5 0.4 copy.14
  14.9 0.4 copy.25
  15.3 0.4 copy.16
  15.7 0.0 copy-done
  15.7 0.5 slice_bitcast_fusion.8
  16.3 1.1 slice_bitcast_fusion
  17.3 1.1 slice_bitcast_fusion.2
  18.4 3.2 %fusion.30 = f32[16,3,1,8,2,256]{5,4,3,1,0,2:T(2,128)S(1)} fusion(f32[16,3,1,8,2,1]{5,4,3,1,0,2:T(2,128)S(1)} %copy.14, f32[16,3,1,8,2,255]{5,4,3,1,0,2:T(2,128)S(1)} %get-tuple-element.141, f32[16,3,1,8,2,255]{5,4,3,1,0,2:T(2,128)S(1)} %get-tuple-element.140, f32[16,3,1,8,2,1]{5,4,3,1,0,2:T(2,128)S(1)} %copy.16, ...), kind=kLoop, calls=%fused_computation.32 | loop fusion | flops 1769472 | bytes 3932160 | tf_op jit(solution)/shard_map/div | solution.py:41
  21.7 0.3 copy.17
  21.9 0.6 div.14
  22.6 0.1 slice_bitcast_fusion.10
  22.7 0.3 slice_bitcast_fusion.6
  23.1 0.4 slice_bitcast_fusion.4
  23.5 1.3 fusion.33
  24.8 0.3 copy.21
  25.2 1.6 %div.17 = f32[16,3,1,4096]{3,0,2,1:T(8,128)} reshape(f32[16,3,1,8,2,256]{5,4,3,0,1,2:T(2,128)S(1)} %copy.21) | data formatting | bytes 1572864 | tf_op jit(solution)/shard_map/div | solution.py:41
  26.8 2.1 %copy.12 = f32[32,3,8,2,256]{4,3,2,0,1:T(2,128)S(1)} copy(f32[32,3,8,2,256]{4,3,2,1,0:T(2,128)} %param.4) | data formatting | bytes 3145728 | tf_op args[0]
  28.9 2.4 %reshape.136 = f32[32,3,4096]{2,0,1:T(8,128)} reshape(f32[32,3,8,2,256]{4,3,2,0,1:T(2,128)S(1)} %copy.12) | data formatting | bytes 3145728 | tf_op jit(solution)/shard_map/reshape | solution.py:54
  31.3 0.0 collective-permute-done
  31.3 0.0 collective-permute-done.1
  31.3 3.9 %fusion.34 = f32[16,3,8,2,256]{4,3,2,1,0:T(2,128)S(1)} fusion(f32[16,3,8,2,256]{4,3,2,1,0:T(2,128)} %collective-permute-done, f32[16,3,8,2,256]{4,3,2,1,0:T(2,128)} %collective-permute-done.1, f32[16,3,8,2,256]{4,3,2,1,0:T(2,128)S(1)} %copy-done), kind=kLoop, calls=%fused_computation.43 | loop fusion | flops 1376256 | bytes 3145728 | tf_op jit(solution)/shard_map/div | solution.py:51
  35.2 0.3 copy.18
  35.6 1.5 stack.8
  37.1 1.5 pad_maximum_fusion
  38.7 62.8 %all-gather.2.cloned.1.call-done = f32[128,3,4096]{2,0,1:T(8,128)} async-done(((f32[16,3,4096]{2,0,1:T(8,128)}), f32[128,3,4096]{2,0,1:T(8,128)}) %all-gather.2.cloned.1.call-update) | async-done | bytes 6291472 | tf_op jit(solution)/shard_map/all_gather | solution.py:75
  101.5 33.1 %while.14 = (s32[]{:T(128)}, f32[32,16,128]{2,1,0:T(8,128)}, f32[32,3,4096]{2,0,1:T(8,128)}, f32[16,3,3,4096]{3,0,2,1:T(8,128)S(1)}, f32[128,3,4096]{2,0,1:T(8,1...) while((s32[]{:T(128)}, f32[32,16,128]{2,1,0:T(8,128)}, ...), condition=%wide.region_1.2_spmd.clone, body=%wide.region_0.1_spmd.clone.sunk | while | flops 4847697920 | bytes 9568473 | solution.py:83
  101.5 0.1 dynamic-slice_bitcast_fusion.8
  101.6 2.1 %dynamic-slice_bitcast_fusion.9 = (f32[32,2048]{1,0:T(8,128)}, f32[32,2048]{1,0:T(8,128)}, f32[32,2048]{1,0:T(8,128)}) fusion(f32[32,3,4096]{2,0,1:T(8,128)} %get-tuple-element.217, s32[]{:T(128)S(6)} %select_n.11, s32[]{:T(128)S(6)} %add.82, s32[]{:T(128)S(6)} %add.83), kind=kLoop, calls=%fused_computation.21.clone.1 | loop fusion | bytes 1572876 | tf_op jit(solution)/shard_map/while/body/eval_jaxpr/mul | solution.py:63
  103.7 14.3 %fusion.41 = f32[32,16,128]{2,1,0:T(8,128)} fusion(f32[128,3,4096]{2,0,1:T(8,128)} %get-tuple-element.219, s32[]{:T(128)S(6)} %select_n.11, f32[16,3,2048]{2,0,1:T(8,128)S(1)} %get-tuple-element.187, f32[32,2048]{1,0:T(8,128)} %get-tuple-element.188, f32[16,3,2048]{2,0,1:T(8,128)S(1)} %get-tuple-element.189, f32[32,2048]{1,0:T(8,128)} %get-tuple-element.190, ...), kind=kOutput, calls=%fused_computation.15.clone.1 | convolution fusion | flops 4847697920 | bytes 5636101 | tf_op jit(solution)/shard_map/while/body/eval_jaxpr/ikbc,jbc->ikj/dot_general | solution.py:69
  118.0 0.1 dynamic-slice_bitcast_fusion.8
  118.1 2.1 %dynamic-slice_bitcast_fusion.9 = (f32[32,2048]{1,0:T(8,128)}, f32[32,2048]{1,0:T(8,128)}, f32[32,2048]{1,0:T(8,128)}) fusion(f32[32,3,4096]{2,0,1:T(8,128)} %get-tuple-element.217, s32[]{:T(128)S(6)} %select_n.11, s32[]{:T(128)S(6)} %add.82, s32[]{:T(128)S(6)} %add.83), kind=kLoop, calls=%fused_computation.21.clone.1 | loop fusion | bytes 1572876 | tf_op jit(solution)/shard_map/while/body/eval_jaxpr/mul | solution.py:63
  120.2 14.3 %fusion.41 = f32[32,16,128]{2,1,0:T(8,128)} fusion(f32[128,3,4096]{2,0,1:T(8,128)} %get-tuple-element.219, s32[]{:T(128)S(6)} %select_n.11, f32[16,3,2048]{2,0,1:T(8,128)S(1)} %get-tuple-element.187, f32[32,2048]{1,0:T(8,128)} %get-tuple-element.188, f32[16,3,2048]{2,0,1:T(8,128)S(1)} %get-tuple-element.189, f32[32,2048]{1,0:T(8,128)} %get-tuple-element.190, ...), kind=kOutput, calls=%fused_computation.15.clone.1 | convolution fusion | flops 4847697920 | bytes 5636101 | tf_op jit(solution)/shard_map/while/body/eval_jaxpr/ikbc,jbc->ikj/dot_general | solution.py:69
  134.6 1.0 broadcast_multiply_fusion
  135.5 12.8 %all_to_all.5 = f32[16,2,16,128]{3,2,1,0:T(8,128)S(1)} all-to-all(f32[16,2,16,128]{3,2,1,0:T(8,128)S(1)} %bitcast.77), channel_id=1, replica_groups=mesh['space'=16,'mode'=8] {'space'}, dimensions={0} | all-to-all | bytes 524288 | tf_op jit(solution)/shard_map/all_to_all | solution.py:34
  148.3 0.6 reduce_sum.9
  (2 shorter events, 0.0 us)
Async XLA Ops:
  6.5 9.2 %copy-start = (f32[16,3,8,2,256]{4,3,2,1,0:T(2,128)S(1)}, f32[16,3,8,2,256]{4,3,2,1,0:T(2,128)}, u32[]{:S(2)}) copy-start(f32[16,3,8,2,256]{4,3,2,1,0:T(2,128)} %param.5) | copy-start | bytes 2359300
  6.5 94.9 %all-gather.2.cloned.1.call-start = ((), (), s32[]{:S(2)}) async-start(), calls=%async_computation.1 | async-start | bytes 7077888 | tf_op jit(solution)/shard_map/all_gather | solution.py:75
  9.7 21.6 %collective-permute-start = (f32[16,3,8,2,256]{4,3,2,1,0:T(2,128)}, f32[16,3,8,2,256]{4,3,2,1,0:T(2,128)}, u32[]{:S(2)}, u32[]{:S(2)}) collective-permute-start(f32[16,3,8,2,256]{4,3,2,1,0:T(2,128)} %param.5), channel_id=1, source_target_pairs={{8,0},{16,8},{24,16},{32,24},{40,32},{48,40},{56,48},{64,56},{72,6... | collective-permute-start | bytes 2359304 | tf_op jit(solution)/shard_map/ppermute | solution.py:21
  11.1 20.2 %collective-permute-start.1 = (f32[16,3,8,2,256]{4,3,2,1,0:T(2,128)}, f32[16,3,8,2,256]{4,3,2,1,0:T(2,128)}, u32[]{:S(2)}, u32[]{:S(2)}) collective-permute-start(f32[16,3,8,2,256]{4,3,2,1,0:T(2,128)} %param.5), channel_id=1, source_target_pairs={{0,8},{8,16},{16,24},{24,32},{32,40},{40,48},{48,56},{56,64},{64,7... | collective-permute-start | bytes 2359304 | tf_op jit(solution)/shard_map/ppermute | solution.py:20
Sparse Core Ops, SparseCore 0:
  9.8 91.6 all-gather.1
where the time goes:
time: 156 us
  waiting for transfers between devices  62.9 us (40%)
  matrix products  28.6 us (18%)
  local copies, waits for them, and re-layouts  23.5 us (15%)
  between operations  13.5 us (9%)
  blocking collectives  12.8 us (8%)
  other arithmetic  11.7 us (8%)
  starting transfers between devices  2.83 us (2%)
    all_gather x1, waiting for transfers between devices, per_device(): everything = lax.all_gather(mode_flat, 'mode', axis=0, tiled=True)  62.8 us
    dot_general x2, matrix products, add_piece(): jnp.einsum('ikbc,jbc->ikj', weighted, piece_block, precision=lax.Precisio...  28.6 us
    all_to_all x1, blocking collectives, sent_and_summed(): lax.all_to_all(parts, axis, split_axis=0, concat_axis=0, tiled=True)  12.8 us
    div x2, other arithmetic, central_diff(): return (8.0 * ahead - farther) / 12.0  4.57 us
    mul x4, local copies, waits for them, and re-layouts, weigh(): weighted = test_block[:, 0, None, None, :] * grad_block[None, :, 0]  4.42 us
    unnamed x6, local copies, waits for them, and re-layouts  4.36 us
    div x1, other arithmetic, per_device(): along_y = (8.0 * ahead - farther) / 12.0  3.94 us
  transfers between devices with their start and end apart: 3, of which 1 were waited for; matrix products, arithmetic and copies ran while one was open for 17% of the time, Pallas kernels for 0%

commit v1 on v0

--- a/solution.py
+++ b/solution.py
@@ -72,7 +72,9 @@
         return running + partial_value
 
     initial = jnp.zeros((test_count, local_count, MODES), jnp.float32)
-    everything = lax.all_gather(mode_flat, "mode", axis=0, tiled=True)
+    everything = jnp.concatenate(
+        lax.all_to_all(jnp.stack([mode_flat] * lax.axis_size("mode")), "mode", 0, 0), axis=0
+    )
 
     def one_block(index_block, running):
         offset = index_block * BLOCK

time: 156 us -> 164 us (1.051)
  between operations: 13.5 us -> 0.17 us
  starting transfers between devices: 2.83 us -> 10.6 us
  local copies, waits for them, and re-layouts: 23.5 us -> 30.7 us
  waiting for transfers between devices: 62.9 us -> 68.3 us
    all_to_all x0 -> x1, waiting for transfers between devices: none -> 68.3 us  [per_device(): lax.all_to_all(jnp.stack([mode_flat] * lax.axis_size('mode')), 'mode', 0, 0)]
    all_gather x1 -> x0, waiting for transfers between devices: 62.8 us -> none  [per_device(): everything = lax.all_gather(mode_flat, 'mode', axis=0, tiled=True)]
    all_to_all x0 -> x1, starting transfers between devices: none -> 8.28 us  [per_device(): lax.all_to_all(jnp.stack([mode_flat] * lax.axis_size('mode')), 'mode', 0, 0)]
    all_to_all x0 -> x1, local copies, waits for them, and re-layouts: none -> 6.14 us  [per_device(): lax.all_to_all(jnp.stack([mode_flat] * lax.axis_size('mode')), 'mode', 0, 0)]
    another operation x0 -> x2, local copies, waits for them, and re-layouts: none -> 4.02 us  [per_device(): jnp.stack([mode_flat] * lax.axis_size('mode'))]
  transfers between devices with their start and end apart: 3 -> 3, of which waited for: 1 -> 1; matrix products, arithmetic and copies ran while one was open for 17% -> 15% of each run, Pallas kernels for 0% -> 0%
where the time goes in v1:
time: 164 us; the launch traced here: 163 us
  waiting for transfers between devices  68.3 us (42%)
  local copies, waits for them, and re-layouts  30.7 us (19%)
  matrix products  28.6 us (17%)
  blocking collectives  13.3 us (8%)
  other arithmetic  11.6 us (7%)
  starting transfers between devices  10.6 us (6%)
    all_to_all x1, waiting for transfers between devices, per_device(): lax.all_to_all(jnp.stack([mode_flat] * lax.axis_size('mode')), 'mode', 0, 0)  68.3 us
    dot_general x2, matrix products, add_piece(): jnp.einsum('ikbc,jbc->ikj', weighted, piece_block, precision=lax.Precisio...  28.6 us
    all_to_all x1, blocking collectives, sent_and_summed(): lax.all_to_all(parts, axis, split_axis=0, concat_axis=0, tiled=True)  13.3 us
    all_to_all x1, starting transfers between devices, per_device(): lax.all_to_all(jnp.stack([mode_flat] * lax.axis_size('mode')), 'mode', 0, 0)  8.28 us
    all_to_all x1, local copies, waits for them, and re-layouts, per_device(): lax.all_to_all(jnp.stack([mode_flat] * lax.axis_size('mode')), 'mode', 0, 0)  6.14 us
    div x2, other arithmetic, central_diff(): return (8.0 * ahead - farther) / 12.0  4.57 us
    mul x4, local copies, waits for them, and re-layouts, weigh(): weighted = test_block[:, 0, None, None, :] * grad_block[None, :, 0]  4.32 us
    unnamed x6, local copies, waits for them, and re-layouts  4.29 us
  transfers between devices with their start and end apart: 3, of which 1 were waited for; matrix products, arithmetic and copies ran while one was open for 15% of the time, Pallas kernels for 0%

profile of v1, /device:TPU:1, one launch (start us, length us, event | category | flops | bytes accessed | tf_op | source)
XLA Modules:
  0.0 163.3 jit_solution(15833085106199229647)
XLA Ops:
  0.0 1.4 copy.44
  1.5 0.6 stack_reshape.2
  2.1 3.4 %stack.13 = f32[8,16,3,4096]{3,1,2,0:T(8,128)} broadcast(f32[16,3,4096]{2,0,1:T(8,128)S(1)} %stack_reshape.2), dimensions={1,2,3} | broadcast | bytes 7077888 | tf_op jit(solution)/shard_map/stack | solution.py:76
  5.5 0.0 copy-start
  5.5 8.3 %all-to-all-start = ((f32[8,16,3,4096]{3,1,2,0:T(8,128)}), f32[8,16,3,4096]{3,1,2,0:T(8,128)}, u32[]{:S(2)}, u32[]{:S(2)}) async-start(f32[8,16,3,4096]{3,1,2,0:T(8,128)} %stack.13), calls=%async_computation | async-start | bytes 12582912 | tf_op jit(solution)/shard_map/all_to_all | solution.py:76
  13.8 0.0 copy-done
  13.8 1.0 collective-permute-start
  14.8 1.3 collective-permute-start.1
  16.1 0.5 fusion.35
  16.6 0.4 copy.47
  17.0 0.4 copy.36
  17.4 0.4 copy.48
  17.8 0.4 copy.38
  18.2 0.5 slice_bitcast_fusion.8
  18.7 1.1 slice_bitcast_fusion
  19.8 1.1 slice_bitcast_fusion.2
  20.9 3.2 %fusion.30 = f32[16,3,1,8,2,256]{5,4,3,1,0,2:T(2,128)S(1)} fusion(f32[16,3,1,8,2,1]{5,4,3,1,0,2:T(2,128)S(1)} %copy.36, f32[16,3,1,8,2,255]{5,4,3,1,0,2:T(2,128)S(1)} %get-tuple-element.141, f32[16,3,1,8,2,255]{5,4,3,1,0,2:T(2,128)S(1)} %get-tuple-element.140, f32[16,3,1,8,2,1]{5,4,3,1,0,2:T(2,128)S(1)} %copy.38, ...), kind=kLoop, calls=%fused_computation.32 | loop fusion | flops 1769472 | bytes 3932160 | tf_op jit(solution)/shard_map/div | solution.py:41
  24.1 0.3 copy.39
  24.4 0.6 div.14
  25.1 0.1 slice_bitcast_fusion.10
  25.2 0.3 slice_bitcast_fusion.6
  25.6 0.4 slice_bitcast_fusion.4
  26.0 1.3 fusion.33
  27.3 0.3 copy.43
  27.6 1.5 div.17
  29.2 2.1 %copy.34 = f32[32,3,8,2,256]{4,3,2,0,1:T(2,128)S(1)} copy(f32[32,3,8,2,256]{4,3,2,1,0:T(2,128)} %param.4) | data formatting | bytes 3145728 | tf_op args[0]
  31.3 2.4 %reshape.138 = f32[32,3,4096]{2,0,1:T(8,128)} reshape(f32[32,3,8,2,256]{4,3,2,0,1:T(2,128)S(1)} %copy.34) | data formatting | bytes 3145728 | tf_op jit(solution)/shard_map/reshape | solution.py:54
  33.7 0.0 collective-permute-done
  33.7 0.0 collective-permute-done.1
  33.7 3.9 %fusion.34 = f32[16,3,8,2,256]{4,3,2,1,0:T(2,128)S(1)} fusion(f32[16,3,8,2,256]{4,3,2,1,0:T(2,128)} %collective-permute-done, f32[16,3,8,2,256]{4,3,2,1,0:T(2,128)} %collective-permute-done.1, f32[16,3,8,2,256]{4,3,2,1,0:T(2,128)S(1)} %copy-done), kind=kLoop, calls=%fused_computation.43 | loop fusion | flops 1376256 | bytes 3145728 | tf_op jit(solution)/shard_map/div | solution.py:51
  37.6 0.3 copy.40
  37.9 1.5 stack.11
  39.4 1.5 pad_maximum_fusion
  41.0 68.3 %all-to-all-done = f32[8,16,3,4096]{3,1,2,0:T(8,128)} async-done(((f32[8,16,3,4096]{3,1,2,0:T(8,128)}), f32[8,16,3,4096]{3,1,2,0:T(8,128)}, u32[]{:S(2)}, u32[]{:S(2)}) %all-to-all-start) | async-done | bytes 6291488 | tf_op jit(solution)/shard_map/all_to_all | solution.py:76
  109.3 6.1 %copy.45 = f32[8,16,3,4096]{3,1,0,2:T(8,128)} copy(f32[8,16,3,4096]{3,1,2,0:T(8,128)} %all-to-all-done) | data formatting | bytes 12582912 | tf_op jit(solution)/shard_map/all_to_all | solution.py:76
  115.4 32.9 %while.14 = (s32[]{:T(128)}, f32[32,16,128]{2,1,0:T(8,128)}, f32[32,3,4096]{2,0,1:T(8,128)}, f32[16,3,3,4096]{3,0,2,1:T(8,128)S(1)}, f32[128,3,4096]{2,0,1:T(8,1...) while((s32[]{:T(128)}, f32[32,16,128]{2,1,0:T(8,128)}, ...), condition=%wide.region_1.2_spmd.clone, body=%wide.region_0.1_spmd.clone.sunk | while | flops 4847697920 | bytes 9568473 | solution.py:85
  115.4 0.1 dynamic-slice_bitcast_fusion.8
  115.5 2.1 %dynamic-slice_bitcast_fusion.9 = (f32[32,2048]{1,0:T(8,128)}, f32[32,2048]{1,0:T(8,128)}, f32[32,2048]{1,0:T(8,128)}) fusion(f32[32,3,4096]{2,0,1:T(8,128)} %get-tuple-element.217, s32[]{:T(128)S(6)} %select_n.11, s32[]{:T(128)S(6)} %add.82, s32[]{:T(128)S(6)} %add.83), kind=kLoop, calls=%fused_computation.21.clone.1 | loop fusion | bytes 1572876 | tf_op jit(solution)/shard_map/while/body/eval_jaxpr/mul | solution.py:63
  117.6 14.3 %fusion.41 = f32[32,16,128]{2,1,0:T(8,128)} fusion(f32[128,3,4096]{2,0,1:T(8,128)} %get-tuple-element.219, s32[]{:T(128)S(6)} %select_n.11, f32[16,3,2048]{2,0,1:T(8,128)S(1)} %get-tuple-element.187, f32[32,2048]{1,0:T(8,128)} %get-tuple-element.188, f32[16,3,2048]{2,0,1:T(8,128)S(1)} %get-tuple-element.189, f32[32,2048]{1,0:T(8,128)} %get-tuple-element.190, ...), kind=kOutput, calls=%fused_computation.15.clone.1 | convolution fusion | flops 4847697920 | bytes 5636101 | tf_op jit(solution)/shard_map/while/body/eval_jaxpr/ikbc,jbc->ikj/dot_general | solution.py:69
  131.9 0.1 dynamic-slice_bitcast_fusion.8
  132.0 2.1 %dynamic-slice_bitcast_fusion.9 = (f32[32,2048]{1,0:T(8,128)}, f32[32,2048]{1,0:T(8,128)}, f32[32,2048]{1,0:T(8,128)}) fusion(f32[32,3,4096]{2,0,1:T(8,128)} %get-tuple-element.217, s32[]{:T(128)S(6)} %select_n.11, s32[]{:T(128)S(6)} %add.82, s32[]{:T(128)S(6)} %add.83), kind=kLoop, calls=%fused_computation.21.clone.1 | loop fusion | bytes 1572876 | tf_op jit(solution)/shard_map/while/body/eval_jaxpr/mul | solution.py:63
  134.1 14.3 %fusion.41 = f32[32,16,128]{2,1,0:T(8,128)} fusion(f32[128,3,4096]{2,0,1:T(8,128)} %get-tuple-element.219, s32[]{:T(128)S(6)} %select_n.11, f32[16,3,2048]{2,0,1:T(8,128)S(1)} %get-tuple-element.187, f32[32,2048]{1,0:T(8,128)} %get-tuple-element.188, f32[16,3,2048]{2,0,1:T(8,128)S(1)} %get-tuple-element.189, f32[32,2048]{1,0:T(8,128)} %get-tuple-element.190, ...), kind=kOutput, calls=%fused_computation.15.clone.1 | convolution fusion | flops 4847697920 | bytes 5636101 | tf_op jit(solution)/shard_map/while/body/eval_jaxpr/ikbc,jbc->ikj/dot_general | solution.py:69
  148.3 1.0 broadcast_multiply_fusion
  149.3 13.3 %all_to_all.10 = f32[16,2,16,128]{3,2,1,0:T(8,128)S(1)} all-to-all(f32[16,2,16,128]{3,2,1,0:T(8,128)S(1)} %bitcast.79), channel_id=1, replica_groups=mesh['space'=16,'mode'=8] {'space'}, dimensions={0} | all-to-all | bytes 524288 | tf_op jit(solution)/shard_map/all_to_all | solution.py:34
  162.6 0.6 reduce_sum.9
  (2 shorter events, 0.0 us)
Async XLA Ops:
  5.5 8.3 %copy-start = (f32[16,3,8,2,256]{4,3,2,1,0:T(2,128)S(1)}, f32[16,3,8,2,256]{4,3,2,1,0:T(2,128)}, u32[]{:S(2)}) copy-start(f32[16,3,8,2,256]{4,3,2,1,0:T(2,128)} %param.5) | copy-start | bytes 2359300
  5.5 103.8 %all-to-all-start = ((f32[8,16,3,4096]{3,1,2,0:T(8,128)}), f32[8,16,3,4096]{3,1,2,0:T(8,128)}, u32[]{:S(2)}, u32[]{:S(2)}) async-start(f32[8,16,3,4096]{3,1,2,0:T(8,128)} %stack.13), calls=%async_computation | async-start | bytes 12582912 | tf_op jit(solution)/shard_map/all_to_all | solution.py:76
  13.8 19.9 %collective-permute-start = (f32[16,3,8,2,256]{4,3,2,1,0:T(2,128)S(1)}, f32[16,3,8,2,256]{4,3,2,1,0:T(2,128)}, u32[]{:S(2)}, u32[]{:S(2)}) collective-permute-start(f32[16,3,8,2,256]{4,3,2,1,0:T(2,128)S(1)} %copy-done), channel_id=1, source_target_pairs={{8,0},{16,8},{24,16},{32,24},{40,32},{48,40},{56,48},{64,56},{72,6... | collective-permute-start | bytes 2359304 | tf_op jit(solution)/shard_map/ppermute | solution.py:21
  14.8 18.9 %collective-permute-start.1 = (f32[16,3,8,2,256]{4,3,2,1,0:T(2,128)S(1)}, f32[16,3,8,2,256]{4,3,2,1,0:T(2,128)}, u32[]{:S(2)}, u32[]{:S(2)}) collective-permute-start(f32[16,3,8,2,256]{4,3,2,1,0:T(2,128)S(1)} %copy-done), channel_id=1, source_target_pairs={{0,8},{8,16},{16,24},{24,32},{32,40},{40,48},{48,56},{56,64},{64,7... | collective-permute-start | bytes 2359304 | tf_op jit(solution)/shard_map/ppermute | solution.py:20
